TPU v7x, 32 devices: a whole 2x2x4 slice. The times are simulated.
32 devices in a mesh: shard: 32 (over z, y, x, core).
Axes of the slice: x: 2, y: 2, z: 4, core: 2. Of those that a mesh axis runs over, the one named last changes fastest.
Arguments:
- data_t: bfloat16 [8192, 8192], P('shard'), may hold values from -0.125 to 0.125
- labels: int32 [8192], replicated, may hold values from -1 to 1, as said below
- sample_weight: float32 [8192], replicated, may hold values from 0.1 to 4
- w_start: float32 [8192], P('shard'), may hold values from -10 to 10
- alpha_start: float32 [8192], P('shard'), may hold values from 0 to 1
- visit_order: int32 [64, 128], P('shard'), may hold values from 0 to 127, each once within a row
Outputs:
- weights_out: float32 [8192], P('shard')
- alpha_final: float32 [8192], P('shard')
- objective: float32 [], replicated
Inputs may be any that keep to these rules, and one draw needn't show every extreme that they name: `labels`: each label is -1 or +1. `visit_order`: each row is a permutation of 0 to 127.
All inputs are finite; a program needn't handle non-finite values.
Results may differ from a plain program's by a relative error of at most 0.0047.
Values may be sent and summed in bfloat16 or wider, within the bound.
A program may use at most 64 MiB of HBM per device.

v0:
```python
import jax
import jax.numpy as jnp
from jax import lax
from jax.sharding import PartitionSpec as P

GROUP = 16


def sweep_rows(gram_block, label_rows, bound_rows, alpha_rows, margin_rows, visit_rows):
    gram_perm = gram_block[visit_rows][:, visit_rows]
    label_perm = label_rows[visit_rows]
    bound_perm = bound_rows[visit_rows]
    alpha_perm = alpha_rows[visit_rows]
    margin_perm = margin_rows[visit_rows]
    diag_perm = jnp.diagonal(gram_perm) + 1e-06

    def update_group(group_index, state_pair):
        alpha_now, margin_now = state_pair
        first_row = jnp.asarray(group_index * GROUP).astype(jnp.int32)
        group_alpha = lax.dynamic_slice_in_dim(alpha_now, first_row, GROUP)
        group_label = lax.dynamic_slice_in_dim(label_perm, first_row, GROUP)
        group_margin = lax.dynamic_slice_in_dim(margin_now, first_row, GROUP)
        group_diag = lax.dynamic_slice_in_dim(diag_perm, first_row, GROUP)
        group_bound = lax.dynamic_slice_in_dim(bound_perm, first_row, GROUP)
        fresh_alpha = jnp.clip(
            group_alpha + (1.0 - group_label * group_margin) / (2.0 * group_diag), 0.0, group_bound
        )
        change = fresh_alpha - group_alpha
        columns = lax.dynamic_slice_in_dim(gram_perm, first_row, GROUP, 1)
        margin_now = margin_now + 2.0 * jnp.dot(
            columns, group_label * change, precision=lax.Precision.HIGHEST
        )
        alpha_now = lax.dynamic_update_slice_in_dim(alpha_now, fresh_alpha, first_row, 0)
        return (alpha_now, margin_now)

    alpha_perm, margin_perm = lax.fori_loop(
        0, alpha_rows.shape[0] // GROUP, update_group, (alpha_perm, margin_perm)
    )
    return jnp.zeros_like(alpha_rows).at[visit_rows].set(alpha_perm)


def body(data_t, labels, sample_weight, w_start, alpha_start, visit_order):
    device_index = lax.axis_index("shard")
    devices = lax.axis_size("shard")
    local_feat = data_t.shape[0]
    samples = labels.shape[0]
    row_count = alpha_start.shape[0]
    features = local_feat * devices
    label_sign = labels.astype(jnp.float32)
    row_first = device_index * row_count
    own_signs = lax.dynamic_slice_in_dim(label_sign, row_first, row_count)
    own_bound = lax.dynamic_slice_in_dim(sample_weight, row_first, row_count)
    relaid = lax.all_to_all(data_t, "shard", split_axis=1, concat_axis=0, tiled=True)
    start_part = jnp.dot(w_start.astype(jnp.bfloat16), data_t, preferred_element_type=jnp.float32)
    start_margin = lax.psum(start_part, "shard")
    weighted = (
        sample_weight * label_sign * jnp.maximum(0.0, 1.0 - label_sign * start_margin)
    ).astype(jnp.bfloat16)
    ascent = jnp.dot(data_t, weighted, preferred_element_type=jnp.float32)
    column_sq = jnp.einsum("fs,fs->f", data_t, data_t, preferred_element_type=jnp.float32)
    scale_col = column_sq / samples + 1e-06
    stepped = w_start + ascent / (samples * scale_col)
    thresh = 1.0 / (4.0 * features * scale_col)
    primal = stepped - jnp.clip(stepped, -thresh, thresh)
    model_part = jnp.dot(primal.astype(jnp.bfloat16), data_t, preferred_element_type=jnp.float32)
    penalty_part = jnp.sum(jnp.abs(primal)) / (4.0 * features)
    own_margin = lax.psum_scatter(model_part, "shard", scatter_dimension=0, tiled=True)
    loss_part = jnp.sum(own_bound * jnp.square(jnp.maximum(0.0, 1.0 - own_signs * own_margin))) / (
        2.0 * samples
    )
    loss_total, penalty = lax.psum((loss_part, penalty_part), "shard")
    objective = loss_total + penalty
    gram_block = lax.dot_general(
        relaid, relaid, (((0,), (0,)), ((), ())), preferred_element_type=jnp.float32
    )
    block_count = visit_order.shape[0]
    visit_rows = (
        visit_order + (jnp.arange(block_count, dtype=jnp.int32) * visit_order.shape[1])[:, None]
    ).reshape(row_count)
    alpha_zero = own_bound * alpha_start
    alpha_one = sweep_rows(gram_block, own_signs, own_bound, alpha_zero, own_margin, visit_rows)
    change_one = (own_signs * (alpha_one - alpha_zero)).astype(jnp.bfloat16)
    update_part = jnp.dot(relaid, change_one, preferred_element_type=jnp.float32) * (2.0 / devices)
    update_one = lax.psum(update_part, "shard")
    second_margin = own_margin + jnp.dot(
        update_one.astype(jnp.bfloat16), relaid, preferred_element_type=jnp.float32
    )
    alpha_two = sweep_rows(gram_block, own_signs, own_bound, alpha_one, second_margin, visit_rows)
    change_two = (own_signs * (alpha_two - alpha_one)).astype(jnp.bfloat16)
    second_part = jnp.dot(relaid, change_two, preferred_element_type=jnp.float32) * (2.0 / devices)
    feat_first = device_index * local_feat
    update_two = lax.psum(second_part, "shard")
    own_two = lax.dynamic_slice_in_dim(update_two, feat_first, local_feat)
    own_one = lax.dynamic_slice_in_dim(update_one, feat_first, local_feat)
    return (primal + own_one + own_two, alpha_two, objective)


def solution(mesh):
    placed = (P("shard", None), P(), P(), P("shard"), P("shard"), P("shard", None))
    return jax.shard_map(
        body, mesh=mesh, in_specs=placed, out_specs=(P("shard"), P("shard"), P()), check_vma=False
    )
```

profile of v0, /device:TPU:14, one launch (start us, length us, event | category | flops | bytes accessed | tf_op | source)
XLA Modules:
  0.0 315.5 jit_solution(12440864550533348112)
XLA Ops:
  0.6 6.4 %copy.19 = bf16[256,8192]{0,1:T(8,128)(2,1)} copy(bf16[256,8192]{1,0:T(8,128)(2,1)} %param.10) | data formatting | bytes 8388608 | tf_op args[0]
  7.0 6.4 %copy.20 = bf16[256,32,256]{2,0,1:T(8,128)(2,1)} copy(bf16[256,32,256]{0,2,1:T(8,128)(2,1)} %bitcast.48) | data formatting | bytes 8388608 | tf_op jit(solution)/shard_map/all_to_all | solution.py:53
  13.4 6.0 %all-to-all-start = ((bf16[256,32,256]{2,0,1:T(8,128)(2,1)}), bf16[256,32,256]{2,0,1:T(8,128)(2,1)}, u32[]{:S(2)}, u32[]{:S(2)}) async-start(bf16[256,32,256]{2,0,1:T(8,128)(2,1)} %copy.20), calls=%async_computation | async-start | bytes 8388608 | tf_op jit(solution)/shard_map/all_to_all | solution.py:53
  19.5 2.8 fusion.28
  22.4 109.1 %psum.35 = f32[8192]{0:T(1024)S(1)} all-reduce(f32[8192]{0:T(1024)S(1)} %bitcast.53), channel_id=1, replica_groups=mesh['shard'=32] {'shard'}, use_global_device_ids=true, to_apply=%region_0.0 | all-reduce | flops 8192 | bytes 65536 | tf_op jit(solution)/shard_map/psum | solution.py:55
  131.5 3.5 %fusion.29 = f32[1,256]{1,0:T(1,128)S(1)} fusion(bf16[8192,1]{0,1:T(2,128)(2,1)S(1)} %reshape.137, bf16[256,8192]{1,0:T(8,128)(2,1)} %param.10), kind=kOutput, calls=%fused_computation.58 | convolution fusion | flops 4194304 | bytes 4211712 | tf_op jit(solution)/shard_map/dot_general | solution.py:59
  135.1 0.9 fusion.16
  136.0 0.6 abs_reduce_fusion
  136.6 2.8 fusion.30
  139.5 42.1 %all-reduce = f32[8192]{0:T(1024)S(1)} all-reduce(f32[8192]{0:T(1024)S(1)} %bitcast.54), channel_id=2, replica_groups=mesh['shard'=32] {'shard'}, use_global_device_ids=true, to_apply=%region_1.2.clone | all-reduce | flops 8192 | bytes 65536
  181.6 0.7 multiply_reduce_fusion
  182.3 1.9 gather_fusion.3
  184.3 1.9 gather_fusion.2
  186.3 1.9 gather_fusion
  188.2 1.9 gather_fusion.1
  191.5 4.7 %fusion.19 = f32[256,256]{1,0:T(8,128)S(1)} fusion(bf16[256,32,256]{2,0,1:T(8,128)(2,1)} %all-to-all-done), kind=kOutput, calls=%fused_computation.35 | convolution fusion | flops 1073741824 | bytes 4456448 | tf_op jit(solution)/shard_map/dot_general | solution.py:73
  196.2 1.0 gather_fusion.4
  197.3 1.0 gather_fusion.5
  198.5 2.4 gather_fusion.6
  200.8 8.5 %while.30 = (s32[]{:T(128)}, f32[256]{0:T(256)S(1)}, f32[256]{0:T(256)S(1)}, f32[256]{0:T(256)S(1)}, f32[256]{0:T(256)S(1)}, /*index=5*/f32[256]{0:T(256)S(1)}, ...) while((s32[]{:T(128)}, f32[256]{0:T(256)S(1)}, f32[256]{0:T(256)S(1)}, ...), condition=%wide.region_3.4_spmd, body=%wide.region_2.3_spmd.sunk | while | flops 49814 | bytes 145567 | solution.py:36
  200.9 0.2 fusion.56
  201.1 0.2 fusion.57
  201.6 0.2 fusion.57
  202.1 0.2 fusion.57
  202.6 0.2 fusion.57
  203.2 0.2 fusion.57
  203.7 0.2 fusion.57
  204.2 0.2 fusion.57
  204.8 0.2 fusion.57
  205.3 0.2 fusion.57
  205.8 0.2 fusion.57
  206.4 0.2 fusion.57
  206.9 0.2 fusion.57
  207.4 0.2 fusion.57
  207.9 0.2 fusion.57
  208.5 0.2 fusion.57
  209.0 0.2 fusion.57
  209.3 1.4 scatter_custom_fusion
  210.7 1.9 gather_fusion.7
  212.7 3.4 %fusion.31 = f32[1,8192]{1,0:T(1,128)S(1)} fusion(bf16[256,1]{0,1:T(2,128)(2,1)S(1)} %reshape.144, bf16[8192,256]{1,0:T(8,128)(2,1)} %bitcast.14), kind=kOutput, calls=%fused_computation.60 | convolution fusion | flops 4194304 | bytes 4227584 | tf_op jit(solution)/shard_map/dot_general | solution.py:83
  216.1 38.4 %psum.36 = f32[8192]{0:T(1024)S(1)} all-reduce(f32[8192]{0:T(1024)S(1)} %broadcast_multiply_fusion.1), channel_id=1, replica_groups=mesh['shard'=32] {'shard'}, use_global_device_ids=true, to_apply=%region_5.6 | all-reduce | flops 8192 | bytes 65536 | tf_op jit(solution)/shard_map/psum | solution.py:84
  254.5 2.8 fusion.32
  257.4 2.0 gather_fusion.8
  259.3 8.5 %while.31 = (s32[]{:T(128)}, f32[256]{0:T(256)S(1)}, f32[256]{0:T(256)S(1)}, f32[256]{0:T(256)S(1)}, f32[256]{0:T(256)S(1)}, /*index=5*/f32[256]{0:T(256)S(1)}, ...) while((s32[]{:T(128)}, f32[256]{0:T(256)S(1)}, f32[256]{0:T(256)S(1)}, ...), condition=%wide.region_7.8_spmd, body=%wide.region_6.7_spmd.sunk | while | flops 49814 | bytes 145567 | solution.py:36
  259.5 0.2 fusion.61
  260.0 0.2 fusion.61
  260.6 0.2 fusion.61
  261.1 0.2 fusion.61
  261.6 0.2 fusion.61
  262.2 0.2 fusion.61
  262.7 0.2 fusion.61
  263.2 0.2 fusion.61
  263.8 0.2 fusion.61
  264.3 0.2 fusion.61
  264.8 0.2 fusion.61
  265.3 0.2 fusion.61
  265.9 0.2 fusion.61
  266.4 0.2 fusion.61
  266.9 0.2 fusion.61
  267.5 0.2 fusion.61
  267.8 1.4 scatter_custom_fusion.1
  269.2 3.4 %fusion.33 = f32[1,8192]{1,0:T(1,128)S(1)} fusion(bf16[256,1]{0,1:T(2,128)(2,1)S(1)} %reshape.148, bf16[8192,256]{1,0:T(8,128)(2,1)} %bitcast.14), kind=kOutput, calls=%fused_computation.62 | convolution fusion | flops 4194304 | bytes 4227584 | tf_op jit(solution)/shard_map/dot_general | solution.py:90
  272.6 42.2 %all-reduce.1 = (f32[8192]{0:T(1024)S(1)}, f32[]{:T(128)}) all-reduce(f32[8192]{0:T(1024)S(1)} %broadcast_multiply_fusion, f32[]{:T(128)S(6)} %add.173), channel_id=1, replica_groups=mesh['shard'=32] {'shard'}, use_global_device_ids=true, to_apply=%region_9.10 | all-reduce | flops 8193 | bytes 65544 | tf_op jit(solution)/shard_map/psum | solution.py:92
  314.8 0.6 dynamic-slice_add_fusion
  (167 shorter events, 7.9 us)
Async XLA Ops:
  13.4 6.1 %copy-start.6 = (f32[256]{0:T(256)S(1)}, f32[256]{0:T(256)}, u32[]{:S(2)}) copy-start(f32[256]{0:T(256)} %param.13) | copy-start | bytes 3076
  13.4 6.1 %copy-start.1 = (s32[8192]{0:T(1024)S(1)}, s32[8192]{0:T(1024)}, u32[]{:S(2)}) copy-start(s32[8192]{0:T(1024)} %param.11) | copy-start | bytes 98308
  13.4 178.0 %all-to-all-start = ((bf16[256,32,256]{2,0,1:T(8,128)(2,1)}), bf16[256,32,256]{2,0,1:T(8,128)(2,1)}, u32[]{:S(2)}, u32[]{:S(2)}) async-start(bf16[256,32,256]{2,0,1:T(8,128)(2,1)} %copy.20), calls=%async_computation | async-start | bytes 8388608 | tf_op jit(solution)/shard_map/all_to_all | solution.py:53
  19.5 112.0 %copy-start.2 = (f32[8192]{0:T(1024)S(1)}, f32[8192]{0:T(1024)}, u32[]{:S(2)}) copy-start(f32[8192]{0:T(1024)} %param.12) | copy-start | bytes 98308
  131.5 3.6 %copy-start = (bf16[256,8192]{1,0:T(8,128)(2,1)S(1)}, bf16[256,8192]{1,0:T(8,128)(2,1)}, u32[]{:S(2)}) copy-start(bf16[256,8192]{1,0:T(8,128)(2,1)} %param.10) | copy-start | bytes 12582916
  135.1 47.2 %copy-start.5 = (s32[2,128]{1,0:T(2,128)S(1)}, s32[2,128]{1,0:T(2,128)}, u32[]{:S(2)}) copy-start(s32[2,128]{1,0:T(2,128)} %param.15) | copy-start | bytes 3076
  136.0 50.2 %copy-start.3 = (f32[256]{0:T(256)S(1)}, f32[256]{0:T(256)}, u32[]{:S(2)}) copy-start(f32[256]{0:T(256)} %param.14) | copy-start | bytes 3076
  269.2 46.3 %copy-start.4 = (f32[256]{0:T(256)}, f32[256]{0:T(256)S(1)}, u32[]{:S(2)}) copy-start(f32[256]{0:T(256)S(1)} %scatter_custom_fusion.1) | copy-start | bytes 3076
where the time goes:
time: 316 us; the launch traced here: 315 us
  blocking collectives  232 us (73%)
  local copies, waits for them, and re-layouts  32.1 us (10%)
  matrix products  31.5 us (10%)
  other arithmetic  10.4 us (3%)
  starting transfers between devices  6.02 us (2%)
    psum x1, blocking collectives, body(): start_margin = lax.psum(start_part, 'shard')  109 us
    psum x1, blocking collectives, body(): update_two = lax.psum(second_part, 'shard')  42.2 us
    unnamed x1, blocking collectives  42.1 us
    psum x1, blocking collectives, body(): update_one = lax.psum(update_part, 'shard')  38.4 us
    dot_general x32, matrix products, update_group(): jnp.dot(columns, group_label * change, precision=lax.Precision.HIGHEST)  7.97 us
    unnamed x15, local copies, waits for them, and re-layouts  6.44 us
    all_to_all x1, local copies, waits for them, and re-layouts, body(): lax.all_to_all(data_t, 'shard', split_axis=1, concat_axis=0, tiled=True)  6.41 us
  transfers between devices with their start and end apart: 1, of which 0 were waited for; matrix products, arithmetic and copies ran while one was open for 6% of the time, Pallas kernels for 0%

commit v1 on v0

--- a/solution.py
+++ b/solution.py
@@ -52,7 +52,7 @@
     own_bound = lax.dynamic_slice_in_dim(sample_weight, row_first, row_count)
     relaid = lax.all_to_all(data_t, "shard", split_axis=1, concat_axis=0, tiled=True)
     start_part = jnp.dot(w_start.astype(jnp.bfloat16), data_t, preferred_element_type=jnp.float32)
-    start_margin = lax.psum(start_part, "shard")
+    start_margin = jnp.sum(lax.all_gather(start_part, "shard"), axis=0)
     weighted = (
         sample_weight * label_sign * jnp.maximum(0.0, 1.0 - label_sign * start_margin)
     ).astype(jnp.bfloat16)

time: 316 us -> 300 us (0.949)
  blocking collectives: 232 us -> 124 us
  waiting for transfers between devices: 0.01 us -> 74.6 us
  between operations: 2.28 us -> 15.7 us
    psum x1 -> x0, blocking collectives: 109 us -> none  [body(): start_margin = lax.psum(start_part, 'shard')]
    all_gather x0 -> x1, waiting for transfers between devices: none -> 74.6 us  [body(): start_margin = jnp.sum(lax.all_gather(start_part, 'shard'), axis=0)]
  transfers between devices with their start and end apart: 1 -> 2, of which waited for: 0 -> 1; matrix products, arithmetic and copies ran while one was open for 6% -> 7% of each run, Pallas kernels for 0% -> 0%
where the time goes in v1:
time: 300 us; the launch traced here: 298 us
  blocking collectives  124 us (41%)
  waiting for transfers between devices  74.6 us (25%)
  local copies, waits for them, and re-layouts  33.5 us (11%)
  matrix products  29.9 us (10%)
  between operations  15.7 us (5%)
  other arithmetic  12.7 us (4%)
  starting transfers between devices  6.06 us (2%)
    all_gather x1, waiting for transfers between devices, body(): start_margin = jnp.sum(lax.all_gather(start_part, 'shard'), axis=0)  74.6 us
    unnamed x1, blocking collectives  43.1 us
    psum x1, blocking collectives, body(): update_two = lax.psum(second_part, 'shard')  40.7 us
    psum x1, blocking collectives, body(): update_one = lax.psum(update_part, 'shard')  39.9 us
    dot_general x32, matrix products, update_group(): jnp.dot(columns, group_label * change, precision=lax.Precision.HIGHEST)  7.97 us
    unnamed x15, local copies, waits for them, and re-layouts  6.44 us
    all_to_all x1, local copies, waits for them, and re-layouts, body(): lax.all_to_all(data_t, 'shard', split_axis=1, concat_axis=0, tiled=True)  6.41 us
    all_to_all x1, starting transfers between devices, body(): lax.all_to_all(data_t, 'shard', split_axis=1, concat_axis=0, tiled=True)  6.02 us
  transfers between devices with their start and end apart: 2, of which 1 were waited for; matrix products, arithmetic and copies ran while one was open for 7% of the time, Pallas kernels for 0%

profile of v1, /device:TPU:14, one launch (start us, length us, event | category | flops | bytes accessed | tf_op | source)
XLA Modules:
  0.0 297.6 jit_solution(16320952864683909127)
XLA Ops:
  7.2 6.4 %copy.25 = bf16[256,8192]{0,1:T(8,128)(2,1)} copy(bf16[256,8192]{1,0:T(8,128)(2,1)} %param.10) | data formatting | bytes 8388608 | tf_op args[0]
  13.6 6.4 %copy.26 = bf16[256,32,256]{2,0,1:T(8,128)(2,1)} copy(bf16[256,32,256]{0,2,1:T(8,128)(2,1)} %bitcast.48) | data formatting | bytes 8388608 | tf_op jit(solution)/shard_map/all_to_all | solution.py:53
  20.0 6.0 %all-to-all-start = ((bf16[256,32,256]{2,0,1:T(8,128)(2,1)}), bf16[256,32,256]{2,0,1:T(8,128)(2,1)}, u32[]{:S(2)}, u32[]{:S(2)}) async-start(bf16[256,32,256]{2,0,1:T(8,128)(2,1)} %copy.26), calls=%async_computation | async-start | bytes 8388608 | tf_op jit(solution)/shard_map/all_to_all | solution.py:53
  26.1 3.4 %fusion.28 = f32[1,8192]{1,0:T(1,128)} fusion(bf16[256,1]{0,1:T(2,128)(2,1)S(1)} %reshape.136, bf16[256,8192]{1,0:T(8,128)(2,1)} %param.10), kind=kOutput, calls=%fused_computation.57 | convolution fusion | flops 4194304 | bytes 4227584 | tf_op jit(solution)/shard_map/dot_general | solution.py:54
  29.7 3.1 %fusion.16 = f32[256]{0:T(256)S(1)} fusion(bf16[256,8192]{1,0:T(8,128)(2,1)} %param.10), kind=kLoop, calls=%fused_computation.32 | loop fusion | flops 6291200 | bytes 4195328 | tf_op jit(solution)/shard_map/fs,fs->f/dot_general | solution.py:60
  32.8 74.6 %all-gather.3.cloned.1.call-done = f32[262144]{0:T(1024)} async-done(((f32[8192]{0:T(1024)}), f32[262144]{0:T(1024)}) %all-gather.3.cloned.1.call-update) | async-done | bytes 1048592 | tf_op jit(solution)/shard_map/all_gather | solution.py:55
  107.4 1.4 reshape.131
  109.0 3.5 %fusion.29 = f32[1,256]{1,0:T(1,128)S(1)} fusion(bf16[8192,1]{0,1:T(2,128)(2,1)S(1)} %reshape.138, bf16[256,8192]{1,0:T(8,128)(2,1)} %param.10), kind=kOutput, calls=%fused_computation.58 | convolution fusion | flops 4194304 | bytes 4211712 | tf_op jit(solution)/shard_map/dot_general | solution.py:59
  112.6 0.6 abs_reduce_fusion
  113.2 0.7 fusion.30
  113.9 43.1 %all-reduce = f32[8192]{0:T(1024)S(1)} all-reduce(f32[8192]{0:T(1024)S(1)} %bitcast.54), channel_id=3, replica_groups=mesh['shard'=32] {'shard'}, use_global_device_ids=true, to_apply=%region_1.2.clone | all-reduce | flops 8192 | bytes 65536
  156.9 0.7 multiply_reduce_fusion
  157.6 1.9 gather_fusion.3
  159.6 1.9 gather_fusion.2
  161.5 1.9 gather_fusion
  163.5 1.9 gather_fusion.1
  166.8 4.7 %fusion.19 = f32[256,256]{1,0:T(8,128)S(1)} fusion(bf16[256,32,256]{2,0,1:T(8,128)(2,1)} %all-to-all-done), kind=kOutput, calls=%fused_computation.35 | convolution fusion | flops 1073741824 | bytes 4456448 | tf_op jit(solution)/shard_map/dot_general | solution.py:73
  171.5 1.0 gather_fusion.4
  172.6 1.0 gather_fusion.5
  173.7 2.4 gather_fusion.6
  176.1 8.5 %while.30 = (s32[]{:T(128)}, f32[256]{0:T(256)S(1)}, f32[256]{0:T(256)S(1)}, f32[256]{0:T(256)S(1)}, f32[256]{0:T(256)S(1)}, /*index=5*/f32[256]{0:T(256)S(1)}, ...) while((s32[]{:T(128)}, f32[256]{0:T(256)S(1)}, f32[256]{0:T(256)S(1)}, ...), condition=%wide.region_3.4_spmd, body=%wide.region_2.3_spmd.sunk | while | flops 49814 | bytes 145567 | solution.py:36
  176.3 0.2 fusion.57
  176.8 0.2 fusion.57
  177.4 0.2 fusion.57
  177.9 0.2 fusion.57
  178.4 0.2 fusion.57
  179.0 0.2 fusion.57
  179.5 0.2 fusion.57
  180.0 0.2 fusion.57
  180.6 0.2 fusion.57
  181.1 0.2 fusion.57
  181.6 0.2 fusion.57
  182.1 0.2 fusion.57
  182.7 0.2 fusion.57
  183.2 0.2 fusion.57
  183.7 0.2 fusion.57
  184.3 0.2 fusion.57
  184.6 1.4 scatter_custom_fusion
  186.0 1.9 gather_fusion.7
  188.0 3.4 %fusion.31 = f32[1,8192]{1,0:T(1,128)S(1)} fusion(bf16[256,1]{0,1:T(2,128)(2,1)S(1)} %reshape.145, bf16[8192,256]{1,0:T(8,128)(2,1)} %bitcast.14), kind=kOutput, calls=%fused_computation.60 | convolution fusion | flops 4194304 | bytes 4227584 | tf_op jit(solution)/shard_map/dot_general | solution.py:83
  191.3 39.9 %psum.28 = f32[8192]{0:T(1024)S(1)} all-reduce(f32[8192]{0:T(1024)S(1)} %broadcast_multiply_fusion.1), channel_id=1, replica_groups=mesh['shard'=32] {'shard'}, use_global_device_ids=true, to_apply=%region_5.6 | all-reduce | flops 8192 | bytes 65536 | tf_op jit(solution)/shard_map/psum | solution.py:84
  231.3 2.8 fusion.32
  234.2 2.0 gather_fusion.8
  236.1 8.5 %while.31 = (s32[]{:T(128)}, f32[256]{0:T(256)S(1)}, f32[256]{0:T(256)S(1)}, f32[256]{0:T(256)S(1)}, f32[256]{0:T(256)S(1)}, /*index=5*/f32[256]{0:T(256)S(1)}, ...) while((s32[]{:T(128)}, f32[256]{0:T(256)S(1)}, f32[256]{0:T(256)S(1)}, ...), condition=%wide.region_7.8_spmd, body=%wide.region_6.7_spmd.sunk | while | flops 49814 | bytes 145567 | solution.py:36
  236.3 0.2 fusion.61
  236.9 0.2 fusion.61
  237.4 0.2 fusion.61
  237.9 0.2 fusion.61
  238.5 0.2 fusion.61
  239.0 0.2 fusion.61
  239.5 0.2 fusion.61
  240.0 0.2 fusion.61
  240.6 0.2 fusion.61
  241.1 0.2 fusion.61
  241.6 0.2 fusion.61
  242.2 0.2 fusion.61
  242.7 0.2 fusion.61
  243.2 0.2 fusion.61
  243.8 0.2 fusion.61
  244.3 0.2 fusion.61
  244.6 1.4 scatter_custom_fusion.1
  246.1 3.4 %fusion.33 = f32[1,8192]{1,0:T(1,128)S(1)} fusion(bf16[256,1]{0,1:T(2,128)(2,1)S(1)} %reshape.149, bf16[8192,256]{1,0:T(8,128)(2,1)} %bitcast.14), kind=kOutput, calls=%fused_computation.62 | convolution fusion | flops 4194304 | bytes 4227584 | tf_op jit(solution)/shard_map/dot_general | solution.py:90
  249.4 40.7 %all-reduce.1 = (f32[8192]{0:T(1024)S(1)}, f32[]{:T(128)}) all-reduce(f32[8192]{0:T(1024)S(1)} %broadcast_multiply_fusion, f32[]{:T(128)S(6)} %add.171), channel_id=1, replica_groups=mesh['shard'=32] {'shard'}, use_global_device_ids=true, to_apply=%region_9.10 | all-reduce | flops 8193 | bytes 65544 | tf_op jit(solution)/shard_map/psum | solution.py:92
  290.1 0.6 dynamic-slice_add_fusion
  (171 shorter events, 8.2 us)
Async XLA Ops:
  20.0 6.1 %copy-start.6 = (f32[256]{0:T(256)S(1)}, f32[256]{0:T(256)}, u32[]{:S(2)}) copy-start(f32[256]{0:T(256)} %param.13) | copy-start | bytes 3076
  20.0 146.8 %all-to-all-start = ((bf16[256,32,256]{2,0,1:T(8,128)(2,1)}), bf16[256,32,256]{2,0,1:T(8,128)(2,1)}, u32[]{:S(2)}, u32[]{:S(2)}) async-start(bf16[256,32,256]{2,0,1:T(8,128)(2,1)} %copy.26), calls=%async_computation | async-start | bytes 8388608 | tf_op jit(solution)/shard_map/all_to_all | solution.py:53
  26.0 3.6 %copy-start.1 = (s32[8192]{0:T(1024)S(1)}, s32[8192]{0:T(1024)}, u32[]{:S(2)}) copy-start(s32[8192]{0:T(1024)} %param.11) | copy-start | bytes 98308
  26.0 3.6 %copy-start.5 = (s32[2,128]{1,0:T(2,128)S(1)}, s32[2,128]{1,0:T(2,128)}, u32[]{:S(2)}) copy-start(s32[2,128]{1,0:T(2,128)} %param.15) | copy-start | bytes 3076
  26.0 81.4 %all-gather.3.cloned.1.call-start = ((), (), s32[]{:S(2)}) async-start(), calls=%async_computation.1 | async-start | bytes 1081344 | tf_op jit(solution)/shard_map/all_gather | solution.py:55
  29.6 79.4 %copy-start.2 = (f32[8192]{0:T(1024)S(1)}, f32[8192]{0:T(1024)}, u32[]{:S(2)}) copy-start(f32[8192]{0:T(1024)} %param.12) | copy-start | bytes 98308
  109.0 4.2 %copy-start = (bf16[256,8192]{1,0:T(8,128)(2,1)S(1)}, bf16[256,8192]{1,0:T(8,128)(2,1)}, u32[]{:S(2)}) copy-start(bf16[256,8192]{1,0:T(8,128)(2,1)} %param.10) | copy-start | bytes 12582916
  112.6 49.0 %copy-start.3 = (f32[256]{0:T(256)S(1)}, f32[256]{0:T(256)}, u32[]{:S(2)}) copy-start(f32[256]{0:T(256)} %param.14) | copy-start | bytes 3076
  246.0 44.7 %copy-start.4 = (f32[256]{0:T(256)}, f32[256]{0:T(256)S(1)}, u32[]{:S(2)}) copy-start(f32[256]{0:T(256)S(1)} %scatter_custom_fusion.1) | copy-start | bytes 3076
Sparse Core Ops, SparseCore 0:
  29.7 77.6 all-gather.2
